TPU v7x, 32 devices: a whole 2x2x4 slice. The times are simulated.
32 devices in a mesh: dst: 8 (over z, core), src: 4 (over y, x).
Axes of the slice: x: 2, y: 2, z: 4, core: 2. Of those that a mesh axis runs over, the one named last changes fastest.
Arguments:
- features: bfloat16 [256, 3712], P(('dst', 'src')), may hold values from -6 to 6
- edge_source: int32 [8, 2048], P('dst', 'src'), may hold values from 0 to 255, as said below
- edge_target: int32 [8, 2048], P('dst', 'src'), may hold values from 0 to 255, as said below
- edge_valid: int32 [8, 2048], P('dst', 'src'), may hold values from 0 to 1, as said below
- edge_radial: bfloat16 [8, 2048, 128], P('dst', 'src'), may hold values from -6 to 6
- edge_bias: float32 [8, 8, 2048], P('dst', None, 'src'), may hold values from -10 to 330
- w_radial: bfloat16 [128, 128], replicated, may hold values from -0.5 to 0.5
- w_zero: bfloat16 [896, 896], replicated, may hold values from -0.1875 to 0.1875
- w_one_re: bfloat16 [768, 768], replicated, may hold values from -0.15625 to 0.15625
- w_one_im: bfloat16 [768, 768], replicated, may hold values from -0.15625 to 0.15625
- w_two_re: bfloat16 [640, 640], replicated, may hold values from -0.15625 to 0.15625
- w_two_im: bfloat16 [640, 640], replicated, may hold values from -0.15625 to 0.15625
- att_vector: float32 [128], replicated, may hold values from -3 to 3
- w_out: bfloat16 [7, 128, 128], replicated, may hold values from -0.5 to 0.5
Outputs:
- attended: bfloat16 [256, 3712], P(('dst', 'src'))
Inputs may be any that keep to these rules, and one draw needn't show every extreme that they name: `edge_source`: in row d, column block s (the tile of destination block d and source block s) every entry is an atom a with (a // 8) % 4 == s. `edge_target`: in row d every entry lies in [d * 8 * 4, (d + 1) * 8 * 4); every atom is the target of at least one valid slot. `edge_valid`: about five sixteenths of the slots are valid.
All inputs are finite; a program needn't handle non-finite values.
Results may differ from a plain program's by a relative error of at most 0.0093.
Values may be sent and summed in bfloat16 or wider, within the bound.
A program may use at most 128 MiB of HBM per device.

v0:
```python
import jax
import jax.numpy as jnp
import numpy as np
from jax import lax
from jax.sharding import PartitionSpec as P

HEADS = 8
NCOEF = 29


NEG = -1e30


def merged_2(part, axis, combine):
    gathered = jax.tree.map(lambda a: lax.all_gather(a, axis), part)

    def take(source):
        return jax.tree.map(lambda a: lax.dynamic_index_in_dim(a, source, 0, False), gathered)

    return lax.fori_loop(
        1, lax.axis_size(axis), lambda source, state: combine(state, take(source)), take(0)
    )


def product(left, right):
    return jnp.dot(left, right, preferred_element_type=jnp.float32)


def exact_product(left, right):
    return jnp.dot(left, right, precision=lax.Precision.HIGHEST, preferred_element_type=jnp.float32)


def spread_heads(weights, copies, channels):
    return jnp.tile(jnp.repeat(weights, channels // weights.shape[1], axis=1), (1, copies))


def degree_table():
    return np.array(list(range(7)) + list(range(1, 7)) * 2 + list(range(2, 7)) * 2, dtype=np.int32)


def edge_messages(rows, gain, w_zero, w_one_re, w_one_im, w_two_re, w_two_im, att_vector):
    channels = gain.shape[1]
    count = rows.shape[0]

    def part(low, high):
        return (
            rows[:, low * channels : high * channels].astype(jnp.float32)
            * jnp.tile(gain, (1, high - low))
        ).astype(jnp.bfloat16)

    zero = part(0, 7)
    up_one, uq_one = (part(7, 13), part(13, 19))
    up_two, uq_two = (part(19, 24), part(24, 29))
    out_zero = product(zero, w_zero)
    yp_one = product(up_one, w_one_re) - product(uq_one, w_one_im)
    yq_one = product(up_one, w_one_im) + product(uq_one, w_one_re)
    yp_two = product(up_two, w_two_re) - product(uq_two, w_two_im)
    yq_two = product(up_two, w_two_im) + product(uq_two, w_two_re)
    active = jax.nn.silu(out_zero[:, :channels]) * att_vector[None, :]
    logit = active.reshape(count, HEADS, channels // HEADS).sum(axis=2)
    values = jnp.concatenate([out_zero, yp_one, yq_one, yp_two, yq_two], axis=1)
    return (logit, values)


def shards(
    features,
    edge_source,
    edge_target,
    edge_valid,
    edge_radial,
    edge_bias,
    w_radial,
    w_zero,
    w_one_re,
    w_one_im,
    w_two_re,
    w_two_im,
    att_vector,
    w_out,
):
    channels = w_radial.shape[1]
    own_atoms = features.shape[0]
    block_atoms = own_atoms * lax.axis_size("src")
    gathered = lax.all_gather(features, "dst", axis=0, tiled=True)
    source = edge_source[0]
    target = edge_target[0]
    valid = edge_valid[0] > 0
    slots = source.shape[0]
    local_rows = source // block_atoms * own_atoms + source % own_atoms
    rows = jnp.take(gathered, local_rows, axis=0)
    gain = product(edge_radial[0], w_radial)
    logit, values = edge_messages(
        rows, gain, w_zero, w_one_re, w_one_im, w_two_re, w_two_im, att_vector
    )
    logit = logit + edge_bias[0].T
    local_target = target - lax.axis_index("dst") * block_atoms
    member = (
        lax.broadcasted_iota(jnp.int32, (block_atoms, slots), 0) == local_target[None, :]
    ) & valid[None, :]
    one_hot = member.astype(jnp.float32)
    local_top = jnp.max(jnp.where(member[:, :, None], logit[None, :, :], NEG), axis=1)
    edge_top = exact_product(one_hot.T, local_top)
    shifted = jnp.where(valid[:, None], logit - edge_top, 0.0)
    weights = jnp.where(valid[:, None], jnp.exp(shifted), 0.0)
    weighted = values * spread_heads(weights, NCOEF, channels)
    local_den = exact_product(one_hot, weights)
    local_num = exact_product(one_hot, weighted)

    def combine_states(first, second):
        top = jnp.maximum(first[0], second[0])
        scale_first = jnp.exp(first[0] - top)
        scale_second = jnp.exp(second[0] - top)
        den = first[1] * scale_first + second[1] * scale_second
        num = first[2] * spread_heads(scale_first, NCOEF, channels) + second[2] * spread_heads(
            scale_second, NCOEF, channels
        )
        return (top, den, num)

    merged_top, merged_den, merged_num = merged_2(
        (local_top, local_den, local_num), "src", combine_states
    )
    start = lax.axis_index("src") * own_atoms
    own_den = lax.dynamic_slice_in_dim(merged_den, start, own_atoms, 0)
    own_num = lax.dynamic_slice_in_dim(merged_num, start, own_atoms, 0)
    merged = (own_num / spread_heads(own_den, NCOEF, channels)).astype(jnp.bfloat16)
    selected = w_out[degree_table()]
    projected = jnp.einsum(
        "acx,cxy->acy",
        merged.reshape(own_atoms, NCOEF, channels),
        selected,
        preferred_element_type=jnp.float32,
    )
    return projected.astype(jnp.bfloat16).reshape(own_atoms, NCOEF * channels)


def solution(mesh):
    in_specs = (
        P(("dst", "src"), None),
        P("dst", "src"),
        P("dst", "src"),
        P("dst", "src"),
        P("dst", "src", None),
        P("dst", None, "src"),
        P(),
        P(),
        P(),
        P(),
        P(),
        P(),
        P(),
        P(),
    )
    out_specs = P(("dst", "src"), None)
    return jax.shard_map(shards, mesh=mesh, in_specs=in_specs, out_specs=out_specs, check_vma=False)
```

profile of v0, /device:TPU:0, one launch (start us, length us, event | category | flops | bytes accessed | tf_op | source)
XLA Modules:
  0.0 141.0 jit_solution(15630821081774154500)
XLA Ops:
  8.8 1.7 %copy.53 = f32[512,896]{1,0:T(8,128)} copy(f32[512,896]{0,1:T(8,128)S(1)} %bitcast.111) | data formatting | bytes 3670016 | tf_op jit(solution)/shard_map/tile | solution.py:48
  10.5 16.4 %all_gather.21 = bf16[64,3712]{1,0:T(8,128)(2,1)S(1)} all-gather(bf16[8,3712]{1,0:T(8,128)(2,1)S(1)} %copy-done.16), channel_id=1, replica_groups=mesh['dst'=8,'src'=4] {'dst'}, dimensions={0}, use_global_device_ids=true | all-gather | bytes 534528 | tf_op jit(solution)/shard_map/all_gather | solution.py:84
  27.0 4.3 %gather_fusion.1 = bf16[512,3712]{1,0:T(8,128)(2,1)} fusion(bf16[64,3712]{1,0:T(8,128)(2,1)S(1)} %all_gather.21, s32[1024]{0:T(1024)S(1)} %pad_clamp_fusion), kind=kCustom, calls=%fused_computation.1 | custom fusion | bytes 7604224 | tf_op jit(solution)/shard_map/jit(_take)/gather | solution.py:90
  31.3 2.7 %broadcast_select_fusion = bf16[512,3712]{1,0:T(8,128)(2,1)S(1)} fusion(bf16[512,3712]{1,0:T(8,128)(2,1)} %gather_fusion.1, pred[512]{0:T(512)(128)(4,1)S(1)} %compare_and_fusion), kind=kLoop, calls=%fused_computation.13 | loop fusion | flops 1900544 | bytes 7602688 | tf_op jit(solution)/shard_map/jit(_take)/select_n | solution.py:90
  34.0 2.5 %constant_dynamic-update-slice_fusion = (f32[512,3712]{1,0:T(8,128)}, f32[512,896]{1,0:T(8,128)S(1)}) fusion(bf16[896,896]{1,0:T(8,128)(2,1)S(1)} %copy-done, f32[512,896]{1,0:T(8,128)S(1)} %copy-done.5, bf16[512,3712]{1,0:T(8,128)(2,1)S(1)} %broadcast_select_fusion), kind=kOutput, calls=%fused_computation.46 | convolution fusion | flops 823459840 | bytes 8028160 | tf_op jit(solution)/shard_map/dot_general | solution.py:26
  38.8 1.9 %copy.57 = f32[512,768]{1,0:T(8,128)S(1)} copy(f32[512,768]{0,1:T(8,128)} %bitcast.114) | data formatting | bytes 3145728 | tf_op jit(solution)/shard_map/tile | solution.py:48
  40.7 3.6 %fusion.32 = f32[512,768]{1,0:T(8,128)} fusion(bf16[768,768]{1,0:T(8,128)(2,1)} %param.26, f32[512,768]{1,0:T(8,128)S(1)} %copy.57, bf16[512,3712]{1,0:T(8,128)(2,1)} %copy-done.3), kind=kOutput, calls=%fused_computation.80 | convolution fusion | flops 605159424 | bytes 5111808 | tf_op jit(solution)/shard_map/dot_general | solution.py:26
  44.4 3.1 %fusion.31 = f32[512,768]{1,0:T(8,128)} fusion(bf16[768,768]{1,0:T(8,128)(2,1)S(1)} %copy-done.9, f32[512,768]{1,0:T(8,128)S(1)} %copy.57, bf16[512,3712]{1,0:T(8,128)(2,1)} %copy-done.3), kind=kOutput, calls=%fused_computation.79 | convolution fusion | flops 605159424 | bytes 5111808 | tf_op jit(solution)/shard_map/dot_general | solution.py:26
  48.7 2.8 %copy.60 = f32[512,640]{1,0:T(8,128)} copy(f32[512,640]{0,1:T(8,128)} %bitcast.115) | data formatting | bytes 2621440 | tf_op jit(solution)/shard_map/tile | solution.py:48
  51.5 3.7 %fusion.30 = f32[512,640]{1,0:T(8,128)} fusion(bf16[640,640]{1,0:T(8,128)(2,1)} %param.28, f32[512,640]{1,0:T(8,128)} %copy.60, bf16[512,3712]{1,0:T(8,128)(2,1)} %copy-done.3), kind=kOutput, calls=%fused_computation.78 | convolution fusion | flops 420413440 | bytes 4096000 | tf_op jit(solution)/shard_map/dot_general | solution.py:26
  55.2 2.9 %fusion.29 = f32[512,640]{1,0:T(8,128)} fusion(bf16[640,640]{1,0:T(8,128)(2,1)S(1)} %copy-done.13, f32[512,640]{1,0:T(8,128)S(1)} %copy-done.1, bf16[512,3712]{1,0:T(8,128)(2,1)} %copy-done.3), kind=kOutput, calls=%fused_computation.77 | convolution fusion | flops 420413440 | bytes 4096000 | tf_op jit(solution)/shard_map/dot_general | solution.py:26
  58.1 4.0 %tile.110 = f32[512,29,128]{0,2,1:T(8,128)} broadcast(f32[512,128]{0,1:T(8,128)S(1)} %bitcast.117), dimensions={0,2} | broadcast | bytes 7864320 | tf_op jit(solution)/shard_map/tile | solution.py:34
  62.2 8.8 %copy.62 = f32[512,3712]{1,0:T(8,128)} copy(f32[512,3712]{0,1:T(8,128)} %bitcast.110) | data formatting | bytes 15204352 | tf_op jit(solution)/shard_map/tile | solution.py:34
  71.0 4.2 %subtract_dynamic-update-slice_fusion = f32[512,3712]{1,0:T(8,128)} fusion(f32[512,3712]{1,0:T(8,128)} %get-tuple-element.202, f32[512,768]{1,0:T(8,128)} %fusion.32, bf16[768,768]{1,0:T(8,128)(2,1)} %param.27, f32[512,768]{1,0:T(8,128)S(1)} %copy.57, bf16[512,3712]{1,0:T(8,128)(2,1)} %copy-done.3), kind=kOutput, calls=%fused_computation.16 | convolution fusion | flops 605552640 | bytes 6684672 | tf_op jit(solution)/shard_map/dot_general | solution.py:26
  75.2 3.5 %add_dynamic-update-slice_fusion = f32[512,3712]{1,0:T(8,128)} fusion(f32[512,3712]{1,0:T(8,128)} %subtract_dynamic-update-slice_fusion, f32[512,768]{1,0:T(8,128)S(1)} %copy-done.6, bf16[768,768]{1,0:T(8,128)(2,1)} %param.26, f32[512,768]{1,0:T(8,128)S(1)} %copy.57, bf16[512,3712]{1,0:T(8,128)(2,1)S(1)} %copy-done.4), kind=kOutput, calls=%fused_computation.15 | convolution fusion | flops 605552640 | bytes 6684672 | tf_op jit(solution)/shard_map/dot_general | solution.py:26
  78.7 1.9 %fusion.6 = f32[512,3712]{1,0:T(8,128)} fusion(f32[512,3712]{1,0:T(8,128)} %add_dynamic-update-slice_fusion, f32[512,640]{1,0:T(8,128)S(1)} %copy-done.8, bf16[640,640]{1,0:T(8,128)(2,1)S(1)} %copy-done.14, f32[512,640]{1,0:T(8,128)S(1)} %copy-done.2, bf16[512,3712]{1,0:T(8,128)(2,1)S(1)} %copy-done.4), kind=kOutput, calls=%fused_computation.22 | convolution fusion | flops 420741120 | bytes 5406720 | tf_op jit(solution)/shard_map/dot_general | solution.py:26
  80.6 1.9 %fusion.5 = f32[512,3712]{1,0:T(8,128)} fusion(f32[512,3712]{1,0:T(8,128)} %fusion.6, f32[512,640]{1,0:T(8,128)S(1)} %copy-done.7, bf16[640,640]{1,0:T(8,128)(2,1)S(1)} %copy-done.15, f32[512,640]{1,0:T(8,128)S(1)} %copy-done.2, bf16[512,3712]{1,0:T(8,128)(2,1)S(1)} %copy-done.4), kind=kOutput, calls=%fused_computation.20 | convolution fusion | flops 420741120 | bytes 5406720 | tf_op jit(solution)/shard_map/dot_general | solution.py:26
  82.6 7.2 %fusion.3 = f32[32,3712]{1,0:T(8,128)} fusion(f32[512,3712]{1,0:T(8,128)} %fusion.5, f32[512,3712]{1,0:T(8,128)S(1)} %bitcast.109, s32[512]{0:T(512)S(1)} %bitcast.121, pred[512]{0:T(512)(128)(4,1)S(1)} %compare_reduce_fusion), kind=kOutput, calls=%fused_computation.11 | convolution fusion | flops 731742208 | bytes 15682048 | tf_op jit(solution)/shard_map/dot_general | solution.py:30
  91.5 8.2 %all-gather.3 = f32[4,32,8]{1,2,0:T(8,128)S(1)} all-gather(f32[1,32,8]{1,2,0:T(8,128)S(1)} %copy.55), channel_id=2, replica_groups=mesh['dst'=8,'src'=4] {'src'}, dimensions={0}, use_global_device_ids=true | all-gather | bytes 5120 | tf_op jit(solution)/shard_map/all_gather | solution.py:15
  99.8 8.4 %all-gather.4 = f32[4,32,8]{1,2,0:T(8,128)S(1)} all-gather(f32[1,32,8]{1,2,0:T(8,128)S(1)} %convolution_bitcast_fusion), channel_id=3, replica_groups=mesh['dst'=8,'src'=4] {'src'}, dimensions={0}, use_global_device_ids=true | all-gather | bytes 5120 | tf_op jit(solution)/shard_map/all_gather | solution.py:15
  108.2 16.4 %all-gather.7.cloned.1.call-done = f32[128,3712]{1,0:T(8,128)} async-done(((f32[32,3712]{1,0:T(8,128)}), f32[128,3712]{1,0:T(8,128)}) %all-gather.7.cloned.1.call-update) | async-done | bytes 1900560 | tf_op jit(solution)/shard_map/all_gather | solution.py:15
  125.7 5.9 %while.19 = (s32[]{:T(128)}, f32[32,8]{0,1:T(8,128)S(1)}, f32[32,8]{0,1:T(8,128)S(1)}, f32[32,3712]{1,0:T(8,128)S(1)}, f32[4,32,8]{1,2,0:T(8,128)S(1)}, /*index=...) while((s32[]{:T(128)}, f32[32,8]{0,1:T(8,128)S(1)}, ...), condition=%wide.region_3.4_spmd, body=%wide.region_2.3_spmd.sunk | while | flops 357893 | bytes 3467415 | solution.py:20
  126.0 1.7 %fusion.50 = f32[32,3712]{1,0:T(8,128)S(1)} fusion(f32[4,8,29,128]{3,2,1,0:T(8,128)S(1)} %bitcast.106, f32[32,3712]{1,0:T(8,128)S(1)} %get-tuple-element.268, f32[4,8,29,128]{3,2,1,0:T(8,128)S(1)} %bitcast.107, f32[4,32,3712]{2,1,0:T(8,128)} %get-tuple-element.281, s32[]{:T(128)S(6)} %select_n.137), kind=kLoop, calls=%fused_computation.3.clone.1 | loop fusion | flops 356352 | bytes 2375684 | tf_op jit(solution)/shard_map/while/body/eval_jaxpr/add | solution.py:114
  132.0 2.2 %fusion.7 = bf16[8,3712]{1,0:T(8,128)(2,1)} fusion(bf16[29,128,128]{2,1,0:T(8,128)(2,1)} %gather_fusion, f32[32,3712]{1,0:T(8,128)S(1)} %get-tuple-element.182, s32[]{:T(128)S(6)} %select_n.99, f32[8,128]{1,0:T(8,128)S(1)} %tile.112), kind=kOutput, calls=%fused_computation.26 | convolution fusion | flops 7691264 | bytes 1132548 | tf_op jit(solution)/shard_map/acx,cxy->acy/dot_general | solution.py:127
  (104 shorter events, 13.1 us)
Async XLA Ops:
  6.5 27.4 %copy-start = (bf16[896,896]{1,0:T(8,128)(2,1)S(1)}, bf16[896,896]{1,0:T(8,128)(2,1)}, u32[]{:S(2)}) copy-start(bf16[896,896]{1,0:T(8,128)(2,1)} %param.25) | copy-start | bytes 4816900
  6.5 118.1 %all-gather.7.cloned.1.call-start = ((), (), s32[]{:S(2)}) async-start(), calls=%async_computation | async-start | bytes 2375680 | tf_op jit(solution)/shard_map/all_gather | solution.py:15
  8.7 1.7 %copy-start.16 = (bf16[8,3712]{1,0:T(8,128)(2,1)S(1)}, bf16[8,3712]{1,0:T(8,128)(2,1)}, u32[]{:S(2)}) copy-start(bf16[8,3712]{1,0:T(8,128)(2,1)} %param.18) | copy-start | bytes 178180
  8.8 18.1 %copy-start.18 = (s32[1,512]{1,0:T(1,128)S(1)}, s32[1,512]{1,0:T(1,128)}, u32[]{:S(2)}) copy-start(s32[1,512]{1,0:T(1,128)} %param.19) | copy-start | bytes 6148
  31.3 2.7 %copy-start.5 = (f32[512,896]{1,0:T(8,128)S(1)}, f32[512,896]{1,0:T(8,128)}, u32[]{:S(2)}) copy-start(f32[512,896]{1,0:T(8,128)} %copy.53) | copy-start | bytes 5505028
  34.0 2.6 %copy-start.3 = (bf16[512,3712]{1,0:T(8,128)(2,1)}, bf16[512,3712]{1,0:T(8,128)(2,1)S(1)}, u32[]{:S(2)}) copy-start(bf16[512,3712]{1,0:T(8,128)(2,1)S(1)} %broadcast_select_fusion) | copy-start | bytes 11403268
  34.0 2.6 %copy-start.21 = (f32[128]{0:T(128)S(1)}, f32[128]{0:T(128)}, u32[]{:S(2)}) copy-start(f32[128]{0:T(128)} %param.30) | copy-start | bytes 1540
  34.0 2.8 %copy-start.19 = (s32[1,512]{1,0:T(1,128)S(1)}, s32[1,512]{1,0:T(1,128)}, u32[]{:S(2)}) copy-start(s32[1,512]{1,0:T(1,128)} %param.21) | copy-start | bytes 6148
  34.0 2.8 %copy-start.17 = (f32[1,8,512]{2,1,0:T(8,128)S(1)}, f32[1,8,512]{2,1,0:T(8,128)}, u32[]{:S(2)}) copy-start(f32[1,8,512]{2,1,0:T(8,128)} %param.23) | copy-start | bytes 49156
  34.0 2.9 %copy-start.20 = (s32[1,512]{1,0:T(1,128)S(1)}, s32[1,512]{1,0:T(1,128)}, u32[]{:S(2)}) copy-start(s32[1,512]{1,0:T(1,128)} %param.20) | copy-start | bytes 6148
  40.7 3.7 %copy-start.9 = (bf16[768,768]{1,0:T(8,128)(2,1)S(1)}, bf16[768,768]{1,0:T(8,128)(2,1)}, u32[]{:S(2)}) copy-start(bf16[768,768]{1,0:T(8,128)(2,1)} %param.27) | copy-start | bytes 3538948
  51.4 3.7 %copy-start.1 = (f32[512,640]{1,0:T(8,128)S(1)}, f32[512,640]{1,0:T(8,128)}, u32[]{:S(2)}) copy-start(f32[512,640]{1,0:T(8,128)} %copy.60) | copy-start | bytes 3932164
  51.4 3.7 %copy-start.13 = (bf16[640,640]{1,0:T(8,128)(2,1)S(1)}, bf16[640,640]{1,0:T(8,128)(2,1)}, u32[]{:S(2)}) copy-start(bf16[640,640]{1,0:T(8,128)(2,1)} %param.29) | copy-start | bytes 2457604
  71.0 4.2 %copy-start.4 = (bf16[512,3712]{1,0:T(8,128)(2,1)S(1)}, bf16[512,3712]{1,0:T(8,128)(2,1)}, u32[]{:S(2)}) copy-start(bf16[512,3712]{1,0:T(8,128)(2,1)} %copy-done.3) | copy-start | bytes 11403268
  71.0 4.2 %copy-start.6 = (f32[512,768]{1,0:T(8,128)S(1)}, f32[512,768]{1,0:T(8,128)}, u32[]{:S(2)}) copy-start(f32[512,768]{1,0:T(8,128)} %fusion.31) | copy-start | bytes 4718596
  71.0 7.7 %copy-start.8 = (f32[512,640]{1,0:T(8,128)S(1)}, f32[512,640]{1,0:T(8,128)}, u32[]{:S(2)}) copy-start(f32[512,640]{1,0:T(8,128)} %fusion.30) | copy-start | bytes 3932164
  75.2 3.5 %copy-start.2 = (f32[512,640]{1,0:T(8,128)S(1)}, f32[512,640]{1,0:T(8,128)}, u32[]{:S(2)}) copy-start(f32[512,640]{1,0:T(8,128)} %copy.60) | copy-start | bytes 3932164
  75.2 3.5 %copy-start.14 = (bf16[640,640]{1,0:T(8,128)(2,1)S(1)}, bf16[640,640]{1,0:T(8,128)(2,1)}, u32[]{:S(2)}) copy-start(bf16[640,640]{1,0:T(8,128)(2,1)} %param.29) | copy-start | bytes 2457604
  75.2 5.4 %copy-start.15 = (bf16[640,640]{1,0:T(8,128)(2,1)S(1)}, bf16[640,640]{1,0:T(8,128)(2,1)}, u32[]{:S(2)}) copy-start(bf16[640,640]{1,0:T(8,128)(2,1)} %param.28) | copy-start | bytes 2457604
  75.2 7.4 %slice-start = ((s8[7602176]{0:T(1024)(128)(4,1)}), s8[4194304]{0:T(1024)(128)(4,1)S(1)}, s32[]{:S(2)}) async-start(s8[7602176]{0:T(1024)(128)(4,1)} %bitcast.108), calls=%async_computation.1 | async-start | bytes 8388608
  78.7 1.9 %copy-start.7 = (f32[512,640]{1,0:T(8,128)S(1)}, f32[512,640]{1,0:T(8,128)}, u32[]{:S(2)}) copy-start(f32[512,640]{1,0:T(8,128)} %fusion.29) | copy-start | bytes 3932164
  78.7 3.8 %slice-start.1 = ((s8[7602176]{0:T(1024)(128)(4,1)}), s8[3407872]{0:T(1024)(128)(4,1)S(1)}, s32[]{:S(2)}) async-start(s8[7602176]{0:T(1024)(128)(4,1)} %bitcast.108), calls=%async_computation.2 | async-start | bytes 6815744
  82.5 7.3 %copy-start.22 = (s32[29]{0:T(128)S(1)}, s32[29]{0:T(128)}, u32[]{:S(2)}) copy-start(s32[29]{0:T(128)} %constant.134) | copy-start | bytes 352
  82.6 7.3 %copy-start.12 = (bf16[7,128,128]{2,1,0:T(8,128)(2,1)S(1)}, bf16[7,128,128]{2,1,0:T(8,128)(2,1)}, u32[]{:S(2)}) copy-start(bf16[7,128,128]{2,1,0:T(8,128)(2,1)} %param.31) | copy-start | bytes 688132
  (2 other events, 1.7 us)
Sparse Core Ops, SparseCore 0:
  89.9 34.6 all-gather.6
where the time goes:
time: 142 us; the launch traced here: 141 us
  matrix products  38.3 us (27%)
  blocking collectives  33 us (23%)
  local copies, waits for them, and re-layouts  31.2 us (22%)
  waiting for transfers between devices  16.5 us (12%)
  between operations  13.7 us (10%)
  other arithmetic  8.12 us (6%)
    dot_general x10, matrix products, product(): return jnp.dot(left, right, preferred_element_type=jnp.float32)  28.6 us
    all_gather x2, blocking collectives, merged_2(): gathered = jax.tree.map(lambda a: lax.all_gather(a, axis), part)  16.6 us
    all_gather x1, waiting for transfers between devices, merged_2(): gathered = jax.tree.map(lambda a: lax.all_gather(a, axis), part)  16.4 us
    all_gather x1, blocking collectives, shards(): gathered = lax.all_gather(features, 'dst', axis=0, tiled=True)  16.4 us
    another operation x15, local copies, waits for them, and re-layouts, spread_heads(): jnp.tile(jnp.repeat(weights, channels // weights.shape[1], axis=1), (1, c...  13.6 us
    another operation x6, local copies, waits for them, and re-layouts, part(): jnp.tile(gain, (1, high - low))  9.16 us
    dot_general x3, matrix products, exact_product(): jnp.dot(left, right, precision=lax.Precision.HIGHEST, preferred_element_t...  7.55 us
    add x3, other arithmetic, combine_states(): first[2] * spread_heads(scale_first, NCOEF, channels)  5.02 us
  transfers between devices with their start and end apart: 1, of which 1 were waited for; matrix products, arithmetic and copies ran while one was open for 1% of the time, Pallas kernels for 0%

commit v1 on v0

v1 whole, which is shorter than its diff:
```python
import functools

import jax
import jax.numpy as jnp
from jax import lax
from jax.experimental import pallas as pl
from jax.experimental.pallas import tpu as pltpu
from jax.sharding import PartitionSpec as P

HEADS = 8
NEG = -1e30
MESH = pl.DeviceIdType.MESH
CORES = 2
PIECES = ((0, 7), (7, 12), (19, 10))
DEGREES = list(range(7)) + list(range(1, 7)) * 2 + list(range(2, 7)) * 2
F32 = jnp.float32
BF16 = jnp.bfloat16


def dot(left, right):
    return jnp.dot(left, right, preferred_element_type=F32)


def kernel(
    n_dst,
    n_src,
    feat_ref,
    source_ref,
    target_ref,
    valid_ref,
    radial_ref,
    bias_ref,
    w_radial_ref,
    att_ref,
    w_zero_hbm,
    w_one_re_hbm,
    w_one_im_hbm,
    w_two_re_hbm,
    w_two_im_hbm,
    w_out_hbm,
    out_ref,
    w_zero,
    w_one_re,
    w_one_im,
    w_two_re,
    w_two_im,
    w_out,
    feat_buf,
    feat_all,
    gain_ref,
    onehot_ref,
    u_ref,
    weight_ref,
    num_ref,
    send_num,
    recv_num,
    send_stat,
    recv_stat,
    merged_ref,
    load_sem,
    z_send,
    pair_send,
    feat_recv,
    num_send,
    num_recv,
):
    own = feat_ref.shape[0]
    channels = w_radial_ref.shape[1]
    slots = source_ref.shape[1]
    block = own * n_src
    atoms = own * n_dst
    nz = n_dst // CORES
    per_head = channels // HEADS
    d = lax.axis_index("dst")
    s = lax.axis_index("src")
    z = d // CORES
    core = d % CORES
    partner = d + 1 - 2 * core

    def line(j):
        return lax.rem(z + j, nz) * CORES + core

    def other(j):
        return lax.rem(s + j, n_src)

    barrier = pltpu.get_barrier_semaphore()
    for j in range(1, nz):
        pl.semaphore_signal(barrier, inc=1, device_id=(line(j), s), device_id_type=MESH)
    for j in range(1, n_src):
        pl.semaphore_signal(barrier, inc=1, device_id=(d, other(j)), device_id_type=MESH)
    pl.semaphore_signal(barrier, inc=1, device_id=(partner, s), device_id_type=MESH)

    loads = [
        pltpu.make_async_copy(src, dst, load_sem.at[i])
        for i, (src, dst) in enumerate(
            (
                (w_zero_hbm, w_zero),
                (w_one_re_hbm, w_one_re),
                (w_one_im_hbm, w_one_im),
                (w_two_re_hbm, w_two_re),
                (w_two_im_hbm, w_two_im),
                (w_out_hbm, w_out),
            )
        )
    ]
    for load in loads:
        load.start()

    def span(k):
        first, count = PIECES[k]
        return pl.ds(first * channels, count * channels)

    def feature_copy(k, src, index, send, target):
        return pltpu.make_async_remote_copy(
            src_ref=src,
            dst_ref=feat_buf.at[index, :, span(k)],
            send_sem=send,
            recv_sem=feat_recv.at[index, k],
            device_id=(target, s),
            device_id_type=MESH,
        )

    pl.semaphore_wait(barrier, nz - 1 + n_src - 1 + 1)

    started = []
    for k in range(len(PIECES)):
        mine = feat_ref.at[:, span(k)]
        for j in range(1, nz):
            copy = feature_copy(k, mine, d, z_send.at[j, k], line(j))
            copy.start()
            started.append(copy)
        copy = feature_copy(k, mine, d, pair_send.at[0, k], partner)
        copy.start()
        started.append(copy)

    gain_ref[...] = dot(radial_ref[0], w_radial_ref[...])
    source = source_ref[...]
    row = source // block * own + source % own
    picks = lax.broadcasted_iota(jnp.int32, (atoms, slots), 0) == row
    onehot_ref[...] = jnp.transpose(picks.astype(F32)).astype(BF16)

    def relay(k):
        for j in range(1, nz):
            index = line(j)
            feature_copy(k, feat_buf.at[index, :, span(k)], index, z_send.at[j, k], index).wait_recv()
            copy = feature_copy(k, feat_buf.at[index, :, span(k)], index, pair_send.at[j, k], partner)
            copy.start()
            started.append(copy)

    def collect(k):
        mine = pl.ds(pl.multiple_of(d * own, own), own)
        feat_all[mine, span(k)] = feat_ref[:, span(k)].astype(F32)
        for j in range(1, nz):
            index = line(j)
            rows = pl.ds(pl.multiple_of(index * own, own), own)
            feat_all[rows, span(k)] = feat_buf[index, :, span(k)].astype(F32)
        for j in range(nz):
            index = lax.rem(z + j, nz) * CORES + 1 - core
            feature_copy(k, feat_buf.at[index, :, span(k)], index, pair_send.at[j, k], partner).wait_recv()
            rows = pl.ds(pl.multiple_of(index * own, own), own)
            feat_all[rows, span(k)] = feat_buf[index, :, span(k)].astype(F32)

    def spread(k):
        first, count = PIECES[k]
        rows = dot(onehot_ref[...], feat_all[:, span(k)].astype(BF16))
        gain = gain_ref[...]
        for i in range(count):
            at = (first + i) * channels
            u_ref[:, at : at + channels] = (rows[:, i * channels : (i + 1) * channels] * gain).astype(BF16)

    head_of = lax.broadcasted_iota(jnp.int32, (1, channels), 1) // per_head
    together = max(1, 256 // block)
    groups = HEADS // together

    def gather_sums(k, group):
        first, count = PIECES[k]
        rows = pl.ds(group * (together * block), together * block)
        weights = weight_ref[rows, :]
        sums = dot(weights, u_ref[:, span(k)]).astype(BF16)
        if k == 0:
            parts = [dot(sums, w_zero[...])]
        else:
            w_re, w_im = ((w_one_re, w_one_im), (w_two_re, w_two_im))[k - 1]
            half = count // 2 * channels
            plus, minus = sums[:, :half], sums[:, half:]
            parts = [
                dot(plus, w_re[...]) - dot(minus, w_im[...]),
                dot(plus, w_im[...]) + dot(minus, w_re[...]),
            ]
        at = first
        for part in parts:
            for i in range(part.shape[1] // channels):
                columns = pl.ds(at * channels, channels)
                at += 1
                value = part[:, i * channels : (i + 1) * channels]
                total = num_ref[:, columns] if groups > 1 else jnp.zeros((block, channels), F32)
                for j in range(together):
                    head = group * together + j
                    total = jnp.where(head_of == head, value[j * block : (j + 1) * block], total)
                num_ref[:, columns] = total

    def sums_of(k):
        if groups == 1:
            gather_sums(k, 0)
        else:
            lax.fori_loop(0, groups, lambda g, c: (gather_sums(k, g), c)[1], 0)
        first, count = PIECES[k]
        for p in range(n_src):
            send_num[p, :, span(k)] = num_ref[p * own : (p + 1) * own, span(k)].astype(BF16)

    def stat_copy(j, source_at):
        return pltpu.make_async_remote_copy(
            src_ref=send_stat.at[other(j)],
            dst_ref=recv_stat.at[source_at],
            send_sem=num_send.at[j, len(PIECES)],
            recv_sem=num_recv.at[source_at, len(PIECES)],
            device_id=(d, other(j)),
            device_id_type=MESH,
        )

    def num_copy(j, k, source_at):
        return pltpu.make_async_remote_copy(
            src_ref=send_num.at[other(j), :, span(k)],
            dst_ref=recv_num.at[source_at, :, span(k)],
            send_sem=num_send.at[j, k],
            recv_sem=num_recv.at[source_at, k],
            device_id=(d, other(j)),
            device_id_type=MESH,
        )

    def send_sums(k):
        for j in range(1, n_src):
            copy = num_copy(j, k, s)
            copy.start()
            started.append(copy)

    relay(0)
    collect(0)
    spread(0)
    loads[0].wait()
    scalar = dot(u_ref[:, span(0)], w_zero[:, :channels])
    active = scalar / (1.0 + jnp.exp(-scalar))
    att = jnp.where(
        lax.broadcasted_iota(jnp.int32, (HEADS, channels), 0) == head_of, att_ref[...], 0.0
    )
    logit = lax.dot_general(
        att,
        active,
        (((1,), (1,)), ((), ())),
        precision=lax.Precision.HIGHEST,
        preferred_element_type=F32,
    ) + bias_ref[0]
    local_target = target_ref[...] - d * block
    member = (lax.broadcasted_iota(jnp.int32, (block, slots), 0) == local_target) & (valid_ref[...] > 0)
    tops = jnp.zeros((block, channels), F32)
    dens = jnp.zeros((block, channels), F32)
    for h in range(HEADS):
        masked = jnp.where(member, logit[h : h + 1, :], NEG)
        top = jnp.max(masked, axis=1, keepdims=True)
        weight = jnp.where(member, jnp.exp(masked - top), 0.0).astype(BF16)
        weight_ref[h * block : (h + 1) * block, :] = weight
        den = jnp.sum(weight.astype(F32), axis=1, keepdims=True)
        tops = jnp.where(head_of == h, top, tops)
        dens = jnp.where(head_of == h, den, dens)
    for p in range(n_src):
        send_stat[p, :, :channels] = tops[p * own : (p + 1) * own]
        send_stat[p, :, channels:] = dens[p * own : (p + 1) * own]
    relay(1)
    sums_of(0)
    for j in range(1, n_src):
        copy = stat_copy(j, s)
        copy.start()
        started.append(copy)
    send_sums(0)
    collect(1)
    spread(1)
    relay(2)
    loads[1].wait()
    loads[2].wait()
    sums_of(1)
    send_sums(1)
    collect(2)
    spread(2)
    loads[3].wait()
    loads[4].wait()
    sums_of(2)
    send_sums(2)

    for j in range(1, n_src):
        stat_copy(j, other(j)).wait_recv()
    stats = [send_stat[s]] + [recv_stat[other(j)] for j in range(1, n_src)]
    top = functools.reduce(jnp.maximum, [a[:, :channels] for a in stats])
    scales = [jnp.exp(a[:, :channels] - top) for a in stats]
    den = sum(a[:, channels:] * b for a, b in zip(stats, scales))
    inverse = 1.0 / den
    scales = [a * inverse for a in scales]
    loads[5].wait()
    for k, (first, count) in enumerate(PIECES):
        for j in range(1, n_src):
            num_copy(j, k, other(j)).wait_recv()
        for i in range(first, first + count):
            columns = pl.ds(i * channels, channels)
            total = send_num[s, :, columns].astype(F32) * scales[0]
            for j in range(1, n_src):
                total += recv_num[other(j), :, columns].astype(F32) * scales[j]
            merged_ref[i] = total
    for degree in range(w_out_hbm.shape[0]):
        members = [i for i, l in enumerate(DEGREES) if l == degree]
        stacked = jnp.concatenate([merged_ref[i] for i in members], axis=0).astype(BF16)
        result = dot(stacked, w_out[degree])
        for at, i in enumerate(members):
            out_ref[:, i * channels : (i + 1) * channels] = result[at * own : (at + 1) * own].astype(BF16)

    for copy in started:
        copy.wait_send()


def solution(mesh):
    n_dst, n_src = mesh.shape["dst"], mesh.shape["src"]

    def shards(
        features,
        edge_source,
        edge_target,
        edge_valid,
        edge_radial,
        edge_bias,
        w_radial,
        w_zero,
        w_one_re,
        w_one_im,
        w_two_re,
        w_two_im,
        att_vector,
        w_out,
    ):
        own, width = features.shape
        slots = edge_source.shape[1]
        channels = w_radial.shape[1]
        block = own * n_src
        atoms = own * n_dst
        pieces = len(PIECES)
        weights = (w_zero, w_one_re, w_one_im, w_two_re, w_two_im, w_out)
        vmem = pl.BlockSpec(memory_space=pltpu.VMEM)
        hbm = pl.BlockSpec(memory_space=pl.ANY)
        return pl.pallas_call(
            functools.partial(kernel, n_dst, n_src),
            out_shape=jax.ShapeDtypeStruct((own, width), BF16),
            in_specs=[vmem] * 8 + [hbm] * 6,
            out_specs=vmem,
            scratch_shapes=[pltpu.VMEM(w.shape, w.dtype) for w in weights]
            + [
                pltpu.VMEM((n_dst, own, width), BF16),
                pltpu.VMEM((atoms, width), F32),
                pltpu.VMEM((slots, channels), F32),
                pltpu.VMEM((slots, atoms), BF16),
                pltpu.VMEM((slots, width), BF16),
                pltpu.VMEM((HEADS * block, slots), BF16),
                pltpu.VMEM((block, width), F32),
                pltpu.VMEM((n_src, own, width), BF16),
                pltpu.VMEM((n_src, own, width), BF16),
                pltpu.VMEM((n_src, own, 2 * channels), F32),
                pltpu.VMEM((n_src, own, 2 * channels), F32),
                pltpu.VMEM((width // channels, own, channels), F32),
                pltpu.SemaphoreType.DMA((len(weights),)),
                pltpu.SemaphoreType.DMA((n_dst // CORES, pieces)),
                pltpu.SemaphoreType.DMA((n_dst // CORES, pieces)),
                pltpu.SemaphoreType.DMA((n_dst, pieces)),
                pltpu.SemaphoreType.DMA((n_src, pieces + 1)),
                pltpu.SemaphoreType.DMA((n_src, pieces + 1)),
            ],
            compiler_params=pltpu.CompilerParams(
                collective_id=0,
                has_side_effects=True,
                vmem_limit_bytes=60 * 1024 * 1024,
            ),
        )(
            features,
            edge_source,
            edge_target,
            edge_valid,
            edge_radial,
            edge_bias,
            w_radial,
            att_vector.reshape(1, channels),
            *weights,
        )

    in_specs = (
        P(("dst", "src"), None),
        P("dst", "src"),
        P("dst", "src"),
        P("dst", "src"),
        P("dst", "src", None),
        P("dst", None, "src"),
        P(),
        P(),
        P(),
        P(),
        P(),
        P(),
        P(),
        P(),
    )
    out_specs = P(("dst", "src"), None)
    return jax.shard_map(shards, mesh=mesh, in_specs=in_specs, out_specs=out_specs, check_vma=False)
```

time: 142 us -> 25.3 us (0.18)
  matrix products: 38.3 us -> 0 us
  blocking collectives: 33 us -> 0 us
  local copies, waits for them, and re-layouts: 31.2 us -> 1.45 us
  Pallas kernels: 0 us -> 23.6 us
  waiting for transfers between devices: 16.5 us -> 0 us
  between operations: 13.7 us -> 0.01 us
  other arithmetic: 8.12 us -> 0 us
    dot_general x14 -> x0, matrix products: 38.3 us -> none  [the longest x10 28.6 us: product(): return jnp.dot(left, right, preferred_element_type=jnp.float32)]
    all_gather x3 -> x0, blocking collectives: 33 us -> none  [the longest x2 16.6 us: merged_2(): gathered = jax.tree.map(lambda a: lax.all_gather(a, axis), part)]
    pallas_call x0 -> x1, Pallas kernels: none -> 23.6 us  [shards(): pl.pallas_call(functools.partial(kernel, n_dst, n_src), out_shape=jax.Sha...]
    another operation x21 -> x0, local copies, waits for them, and re-layouts: 22.7 us -> none  [the longest x15 13.6 us: spread_heads(): jnp.tile(jnp.repeat(weights, channels // weights.shape[1], axis=1), (1, c...]
    all_gather x1 -> x0, waiting for transfers between devices: 16.4 us -> none  [merged_2(): gathered = jax.tree.map(lambda a: lax.all_gather(a, axis), part)]
    gather x2 -> x0, local copies, waits for them, and re-layouts: 5.93 us -> none  [the longest x1 4.29 us: shards(): rows = jnp.take(gathered, local_rows, axis=0)]
    add x7 -> x0, other arithmetic: 5.08 us -> none  [the longest x3 5.02 us: combine_states(): first[2] * spread_heads(scale_first, NCOEF, channels)]
    select_n x2 -> x0, other arithmetic: 2.69 us -> none  [shards(): rows = jnp.take(gathered, local_rows, axis=0)]
  transfers between devices with their start and end apart: 1 -> 0, of which waited for: 1 -> 0; matrix products, arithmetic and copies ran while one was open for 1% -> 0% of each run, Pallas kernels for 0% -> 0%
where the time goes in v1:
time: 25.3 us; the launch traced here: 25.1 us
  Pallas kernels  23.6 us (93%)
  local copies, waits for them, and re-layouts  1.45 us (6%)
    pallas_call x1, Pallas kernels, shards(): pl.pallas_call(functools.partial(kernel, n_dst, n_src), out_shape=jax.Sha...  23.6 us
    unnamed x1, local copies, waits for them, and re-layouts  1.45 us

profile of v1, /device:TPU:0, one launch (start us, length us, event | category | flops | bytes accessed | tf_op | source)
XLA Modules:
  0.0 25.1 jit_solution(2698099683301782219)
XLA Ops:
  0.0 23.6 %shard_map.136 = bf16[8,3712]{1,0:T(8,128)(2,1)} custom-call(bf16[8,3712]{1,0:T(8,128)(2,1)} %feat_ref.1, s32[1,512]{1,0:T(1,128)} %source_ref.1, s32[1,512]{1,0:T(1,128)} %target_ref.1, s32[1,512]{1,0:T(1,128)} %valid_ref.1, bf16[1,512,128]{2,1,0:T(8,128)(2,1)} %radial_ref.1, f32[1,8,512]{2,1,0:T(8,128)} %bias_ref.1, bf16[128,128]{1,0:T(8,128)(2,1)} %w_radial_ref.1, ...), custom_call_target="tpu_custom_call" | custom-call | tf_op jit(solution)/shard_map/pallas_call | solution.py:346
  23.7 1.5 %copy.16 = bf16[8,3712]{1,0:T(8,128)(2,1)} copy(bf16[8,3712]{1,0:T(8,128)(2,1)} %shard_map.136) | data formatting | bytes 118784

commit v2 on v1

--- a/solution.py
+++ b/solution.py
@@ -24,6 +24,21 @@
 def kernel(
     n_dst,
     n_src,
+    feat_hbm,
+    source_hbm,
+    target_hbm,
+    valid_hbm,
+    radial_hbm,
+    bias_hbm,
+    w_radial_hbm,
+    att_hbm,
+    w_zero_hbm,
+    w_one_re_hbm,
+    w_one_im_hbm,
+    w_two_re_hbm,
+    w_two_im_hbm,
+    w_out_hbm,
+    out_ref,
     feat_ref,
     source_ref,
     target_ref,
@@ -32,13 +47,6 @@
     bias_ref,
     w_radial_ref,
     att_ref,
-    w_zero_hbm,
-    w_one_re_hbm,
-    w_one_im_hbm,
-    w_two_re_hbm,
-    w_two_im_hbm,
-    w_out_hbm,
-    out_ref,
     w_zero,
     w_one_re,
     w_one_im,
@@ -56,7 +64,7 @@
     recv_num,
     send_stat,
     recv_stat,
-    merged_ref,
+    input_sem,
     load_sem,
     z_send,
     pair_send,
@@ -83,6 +91,24 @@
     def other(j):
         return lax.rem(s + j, n_src)
 
+    fetches = [
+        pltpu.make_async_copy(src, dst, input_sem.at[i])
+        for i, (src, dst) in enumerate(
+            (
+                (feat_hbm, feat_ref),
+                (radial_hbm, radial_ref),
+                (w_radial_hbm, w_radial_ref),
+                (source_hbm, source_ref),
+                (target_hbm, target_ref),
+                (valid_hbm, valid_ref),
+                (bias_hbm, bias_ref),
+                (att_hbm, att_ref),
+            )
+        )
+    ]
+    for fetch in fetches:
+        fetch.start()
+
     barrier = pltpu.get_barrier_semaphore()
     for j in range(1, nz):
         pl.semaphore_signal(barrier, inc=1, device_id=(line(j), s), device_id_type=MESH)
@@ -120,6 +146,7 @@
             device_id_type=MESH,
         )
 
+    fetches[0].wait()
     pl.semaphore_wait(barrier, nz - 1 + n_src - 1 + 1)
 
     started = []
@@ -133,6 +160,8 @@
         copy.start()
         started.append(copy)
 
+    for fetch in fetches[1:]:
+        fetch.wait()
     gain_ref[...] = dot(radial_ref[0], w_radial_ref[...])
     source = source_ref[...]
     row = source // block * own + source % own
@@ -298,18 +327,18 @@
     for k, (first, count) in enumerate(PIECES):
         for j in range(1, n_src):
             num_copy(j, k, other(j)).wait_recv()
-        for i in range(first, first + count):
-            columns = pl.ds(i * channels, channels)
-            total = send_num[s, :, columns].astype(F32) * scales[0]
-            for j in range(1, n_src):
-                total += recv_num[other(j), :, columns].astype(F32) * scales[j]
-            merged_ref[i] = total
-    for degree in range(w_out_hbm.shape[0]):
-        members = [i for i, l in enumerate(DEGREES) if l == degree]
-        stacked = jnp.concatenate([merged_ref[i] for i in members], axis=0).astype(BF16)
-        result = dot(stacked, w_out[degree])
-        for at, i in enumerate(members):
-            out_ref[:, i * channels : (i + 1) * channels] = result[at * own : (at + 1) * own].astype(BF16)
+        for degree in sorted(set(DEGREES[first : first + count])):
+            members = [i for i in range(first, first + count) if DEGREES[i] == degree]
+            merged = []
+            for i in members:
+                columns = pl.ds(i * channels, channels)
+                total = send_num[s, :, columns].astype(F32) * scales[0]
+                for j in range(1, n_src):
+                    total += recv_num[other(j), :, columns].astype(F32) * scales[j]
+                merged.append(total)
+            result = dot(jnp.concatenate(merged, axis=0).astype(BF16), w_out[degree])
+            for at, i in enumerate(members):
+                out_ref[:, i * channels : (i + 1) * channels] = result[at * own : (at + 1) * own].astype(BF16)
 
     for copy in started:
         copy.wait_send()
@@ -341,14 +370,25 @@
         atoms = own * n_dst
         pieces = len(PIECES)
         weights = (w_zero, w_one_re, w_one_im, w_two_re, w_two_im, w_out)
+        operands = (
+            features,
+            edge_source,
+            edge_target,
+            edge_valid,
+            edge_radial,
+            edge_bias,
+            w_radial,
+            att_vector.reshape(1, channels),
+            *weights,
+        )
         vmem = pl.BlockSpec(memory_space=pltpu.VMEM)
         hbm = pl.BlockSpec(memory_space=pl.ANY)
         return pl.pallas_call(
             functools.partial(kernel, n_dst, n_src),
             out_shape=jax.ShapeDtypeStruct((own, width), BF16),
-            in_specs=[vmem] * 8 + [hbm] * 6,
+            in_specs=[hbm] * len(operands),
             out_specs=vmem,
-            scratch_shapes=[pltpu.VMEM(w.shape, w.dtype) for w in weights]
+            scratch_shapes=[pltpu.VMEM(w.shape, w.dtype) for w in operands]
             + [
                 pltpu.VMEM((n_dst, own, width), BF16),
                 pltpu.VMEM((atoms, width), F32),
@@ -361,7 +401,7 @@
                 pltpu.VMEM((n_src, own, width), BF16),
                 pltpu.VMEM((n_src, own, 2 * channels), F32),
                 pltpu.VMEM((n_src, own, 2 * channels), F32),
-                pltpu.VMEM((width // channels, own, channels), F32),
+                pltpu.SemaphoreType.DMA((len(operands) - len(weights),)),
                 pltpu.SemaphoreType.DMA((len(weights),)),
                 pltpu.SemaphoreType.DMA((n_dst // CORES, pieces)),
                 pltpu.SemaphoreType.DMA((n_dst // CORES, pieces)),
@@ -374,17 +414,7 @@
                 has_side_effects=True,
                 vmem_limit_bytes=60 * 1024 * 1024,
             ),
-        )(
-            features,
-            edge_source,
-            edge_target,
-            edge_valid,
-            edge_radial,
-            edge_bias,
-            w_radial,
-            att_vector.reshape(1, channels),
-            *weights,
-        )
+        )(*operands)
 
     in_specs = (
         P(("dst", "src"), None),

time: 25.3 us -> 24.4 us (0.964)
  Pallas kernels: 23.6 us -> 22.8 us
    pallas_call x1, Pallas kernels: 23.6 us -> 22.8 us  [shards(): pl.pallas_call(functools.partial(kernel, n_dst, n_src), out_shape=jax.Sha...]
where the time goes in v2:
time: 24.4 us; the launch traced here: 24.3 us
  Pallas kernels  22.8 us (93%)
  local copies, waits for them, and re-layouts  1.45 us (6%)
    pallas_call x1, Pallas kernels, shards(): pl.pallas_call(functools.partial(kernel, n_dst, n_src), out_shape=jax.Sha...  22.8 us
    unnamed x1, local copies, waits for them, and re-layouts  1.45 us

profile of v2, /device:TPU:0, one launch (start us, length us, event | category | flops | bytes accessed | tf_op | source)
XLA Modules:
  0.0 24.3 jit_solution(13404667856272178745)
XLA Ops:
  0.0 22.8 %shard_map.136 = bf16[8,3712]{1,0:T(8,128)(2,1)} custom-call(bf16[8,3712]{1,0:T(8,128)(2,1)} %feat_hbm.1, s32[1,512]{1,0:T(1,128)} %source_hbm.1, s32[1,512]{1,0:T(1,128)} %target_hbm.1, s32[1,512]{1,0:T(1,128)} %valid_hbm.1, bf16[1,512,128]{2,1,0:T(8,128)(2,1)} %radial_hbm.1, f32[1,8,512]{2,1,0:T(8,128)} %bias_hbm.1, bf16[128,128]{1,0:T(8,128)(2,1)} %w_radial_hbm.1, ...), custom_call_target="tpu_custom_call" | custom-call | tf_op jit(solution)/shard_map/pallas_call | solution.py:386
  22.8 1.5 %copy.16 = bf16[8,3712]{1,0:T(8,128)(2,1)} copy(bf16[8,3712]{1,0:T(8,128)(2,1)} %shard_map.136) | data formatting | bytes 118784

commit v3 on v2

--- a/solution.py
+++ b/solution.py
@@ -150,7 +150,8 @@
     pl.semaphore_wait(barrier, nz - 1 + n_src - 1 + 1)
 
     started = []
-    for k in range(len(PIECES)):
+
+    def offer(k):
         mine = feat_ref.at[:, span(k)]
         for j in range(1, nz):
             copy = feature_copy(k, mine, d, z_send.at[j, k], line(j))
@@ -159,6 +160,8 @@
         copy = feature_copy(k, mine, d, pair_send.at[0, k], partner)
         copy.start()
         started.append(copy)
+
+    offer(0)
 
     for fetch in fetches[1:]:
         fetch.wait()
@@ -264,6 +267,8 @@
             started.append(copy)
 
     relay(0)
+    offer(1)
+    offer(2)
     collect(0)
     spread(0)
     loads[0].wait()
@@ -295,11 +300,11 @@
         send_stat[p, :, :channels] = tops[p * own : (p + 1) * own]
         send_stat[p, :, channels:] = dens[p * own : (p + 1) * own]
     relay(1)
-    sums_of(0)
     for j in range(1, n_src):
         copy = stat_copy(j, s)
         copy.start()
         started.append(copy)
+    sums_of(0)
     send_sums(0)
     collect(1)
     spread(1)

time: 24.4 us -> 26.5 us (1.086)
  Pallas kernels: 22.8 us -> 24.9 us
    pallas_call x1, Pallas kernels: 22.8 us -> 24.9 us  [shards(): pl.pallas_call(functools.partial(kernel, n_dst, n_src), out_shape=jax.Sha...]
where the time goes in v3:
time: 26.5 us; the launch traced here: 26.3 us
  Pallas kernels  24.9 us (94%)
  local copies, waits for them, and re-layouts  1.45 us (5%)
    pallas_call x1, Pallas kernels, shards(): pl.pallas_call(functools.partial(kernel, n_dst, n_src), out_shape=jax.Sha...  24.9 us
    unnamed x1, local copies, waits for them, and re-layouts  1.45 us

profile of v3, /device:TPU:0, one launch (start us, length us, event | category | flops | bytes accessed | tf_op | source)
XLA Modules:
  0.0 26.3 jit_solution(4802076623635452040)
XLA Ops:
  0.0 24.9 %shard_map.136 = bf16[8,3712]{1,0:T(8,128)(2,1)} custom-call(bf16[8,3712]{1,0:T(8,128)(2,1)} %feat_hbm.1, s32[1,512]{1,0:T(1,128)} %source_hbm.1, s32[1,512]{1,0:T(1,128)} %target_hbm.1, s32[1,512]{1,0:T(1,128)} %valid_hbm.1, bf16[1,512,128]{2,1,0:T(8,128)(2,1)} %radial_hbm.1, f32[1,8,512]{2,1,0:T(8,128)} %bias_hbm.1, bf16[128,128]{1,0:T(8,128)(2,1)} %w_radial_hbm.1, ...), custom_call_target="tpu_custom_call" | custom-call | tf_op jit(solution)/shard_map/pallas_call | solution.py:391
  24.9 1.5 %copy.16 = bf16[8,3712]{1,0:T(8,128)(2,1)} copy(bf16[8,3712]{1,0:T(8,128)(2,1)} %shard_map.136) | data formatting | bytes 118784
